TPU v7x, 32 devices: a whole 2x2x4 slice. The times are simulated.
32 devices in a mesh: dp: 8 (over z, y), tensor: 4 (over x, core).
Axes of the slice: x: 2, y: 2, z: 4, core: 2. Of those that a mesh axis runs over, the one named last changes fastest.
Arguments:
- cotangent: bfloat16 [2048, 8192], P(('dp', 'tensor')), may hold values from -1.1048543 to 1.1048543
- gate_pre: bfloat16 [2048, 14336], P('dp', 'tensor'), may hold values from -5 to 5
- up_pre: bfloat16 [2048, 14336], P('dp', 'tensor'), may hold values from -28 to 28
- row_state: float32 [8192], P('dp'), may hold values from 0.02 to 3
- column_state: float32 [14336], P('tensor'), may hold values from 0.05 to 2
Outputs:
- update: float32 [8192, 14336], P('dp', 'tensor')
- row_next: float32 [8192], P('dp')
- column_next: float32 [14336], P('tensor')
- row_scale: float32 [1], replicated
All inputs are finite; a program needn't handle non-finite values.
Results may differ from a plain program's by a relative error of at most 0.019.
Values may be sent and summed in bfloat16 or wider, within the bound.
A program may use at most 192 MiB of HBM per device.

v0:
```python
import jax
import jax.numpy as jnp
from jax import lax
from jax.sharding import PartitionSpec as P

D = 8192
FF = 14336
EPSILON = 1e-30
DECAY_RATE = 0.9


def shards(cotangent, gate_pre, up_pre, row_state, column_state):
    hidden = (jax.nn.silu(gate_pre.astype(jnp.float32)) * up_pre.astype(jnp.float32)).astype(
        jnp.bfloat16
    )
    data_count = lax.axis_size("dp")
    tensor_count = lax.axis_size("tensor")
    spread = lax.all_to_all(cotangent, "dp", split_axis=1, concat_axis=0, tiled=True)
    tokens_all = lax.all_gather(spread, "tensor", axis=0, tiled=True)
    rows_each = cotangent.shape[0]
    block_rows = hidden.shape[0]
    blocks = tokens_all.reshape(tensor_count, data_count, rows_each, tokens_all.shape[1])
    incoming = lax.all_gather(hidden, "dp", axis=0, tiled=True)
    groups = incoming.shape[0] // block_rows
    shaped = incoming.reshape(groups, tensor_count, rows_each, incoming.shape[1])
    partial_value = jnp.einsum("jntd,njtf->ndf", blocks, shaped, preferred_element_type=jnp.float32)
    rounded = lax.optimization_barrier(partial_value.astype(jnp.bfloat16))
    gradient = jnp.sum(rounded.astype(jnp.float32), axis=0)
    squares = gradient * gradient + EPSILON
    column_part = jnp.sum(squares, axis=0)
    row_total = lax.psum(jnp.sum(squares, axis=1), "tensor")
    row_next = DECAY_RATE * row_state + (1.0 - DECAY_RATE) * row_total / FF
    column_total = lax.psum(column_part, "dp")
    row_sum_all = lax.psum(jnp.sum(row_next), "dp")
    column_next = DECAY_RATE * column_state + (1.0 - DECAY_RATE) * column_total / D
    row_mean = row_sum_all / D
    second_moment = row_next[:, None] * column_next[None, :] / row_mean
    raw_update = gradient / jnp.sqrt(second_moment)
    square_total = lax.psum(jnp.sum(raw_update * raw_update), ("dp", "tensor"))
    norm_value = jnp.sqrt(square_total / (float(D) * float(FF)))
    update = raw_update / jnp.maximum(1.0, norm_value)
    return (update, row_next, column_next, jnp.reshape(row_mean, (1,)))


def solution(mesh):
    return jax.shard_map(
        shards,
        mesh=mesh,
        in_specs=(
            P(("dp", "tensor"), None),
            P("dp", "tensor"),
            P("dp", "tensor"),
            P("dp"),
            P("tensor"),
        ),
        out_specs=(P("dp", "tensor"), P("dp"), P("tensor"), P()),
        check_vma=False,
    )
```

profile of v0, /device:TPU:12, one launch (start us, length us, event | category | flops | bytes accessed | tf_op | source)
XLA Modules:
  0.0 465.1 jit_solution(13334387134886437163)
XLA Ops:
  7.2 0.0 all-gather.5.cloned.1.call-start
  7.2 1.3 copy.20
  8.5 29.7 %all_to_all.19 = bf16[64,8,1024]{2,0,1:T(8,128)(2,1)} all-to-all(bf16[64,8,1024]{2,0,1:T(8,128)(2,1)S(1)} %bitcast.19), channel_id=1, replica_groups=mesh['dp'=8,'tensor'=4] {'dp'}, dimensions={1} | all-to-all | bytes 2097152 | tf_op jit(solution)/shard_map/all_to_all | solution.py:18
  38.2 0.0 all-gather.5.cloned.1.call-update
  38.2 0.0 all-gather.3.cloned.1.call-start
  38.3 4.4 fusion.8
  42.7 0.0 all-gather.3.cloned.1.call-update
  42.7 30.8 %all-gather.5.cloned.1.call-done = bf16[2048,1024]{1,0:T(8,128)(2,1)} async-done(((bf16[512,1024]{1,0:T(8,128)(2,1)}), bf16[2048,1024]{1,0:T(8,128)(2,1)}) %all-gather.5.cloned.1.call-update) | async-done | bytes 4194320 | tf_op jit(solution)/shard_map/all_gather | solution.py:19
  73.5 201.7 %all-gather.3.cloned.1.call-done = bf16[2048,3584]{1,0:T(8,128)(2,1)} async-done(((bf16[256,3584]{1,0:T(8,128)(2,1)}), bf16[2048,3584]{1,0:T(8,128)(2,1)}) %all-gather.3.cloned.1.call-update) | async-done | bytes 14680080 | tf_op jit(solution)/shard_map/all_gather | solution.py:23
  275.2 28.0 %fusion = bf16[8,1024,3584]{1,2,0:T(8,128)(2,1)} fusion(bf16[8,4,64,3584]{3,2,1,0:T(8,128)(2,1)} %bitcast.21, bf16[4,8,64,1024]{3,2,1,0:T(8,128)(2,1)} %bitcast.22), kind=kOutput, calls=%fused_computation.2 | convolution fusion | flops 15061745664 | bytes 77594624 | tf_op jit(solution)/shard_map/jntd,njtf->ndf/dot_general | solution.py:26
  303.2 24.8 %convert_reduce_fusion = f32[1024,3584]{0,1:T(8,128)} fusion(bf16[8,1024,3584]{1,2,0:T(8,128)(2,1)} %fusion), kind=kLoop, calls=%fused_computation.1 | loop fusion | flops 55050240 | bytes 73400320 | tf_op jit(solution)/shard_map/reduce_sum | solution.py:28
  328.0 7.7 %fusion.1 = (f32[3584]{0:T(1024)S(1)}, f32[1024]{0:T(1024)S(1)}) fusion(f32[1024,3584]{0,1:T(8,128)} %convert_reduce_fusion), kind=kLoop, calls=%fused_computation.6 | loop fusion | flops 14675456 | bytes 14698496 | tf_op jit(solution)/shard_map/reduce_sum | solution.py:30
  335.7 5.9 %psum.28 = f32[1024]{0:T(1024)S(1)} all-reduce(f32[1024]{0:T(1024)S(1)} %get-tuple-element.9), channel_id=1, replica_groups=mesh['dp'=8,'tensor'=4] {'tensor'}, use_global_device_ids=true, to_apply=%region_2.3 | all-reduce | flops 1024 | bytes 8192 | tf_op jit(solution)/shard_map/psum | solution.py:31
  341.5 0.0 copy-done.3
  341.5 0.6 fusion.9
  342.1 32.3 %all-reduce = (f32[]{:T(128)}, f32[3584]{0:T(1024)S(1)}) all-reduce(f32[]{:T(128)} %get-tuple-element.12, f32[3584]{0:T(1024)S(1)} %get-tuple-element.8), channel_id=1, replica_groups=mesh['dp'=8,'tensor'=4] {'dp'}, use_global_device_ids=true, to_apply=%region_6.7 | all-reduce | flops 3585 | bytes 28680 | tf_op jit(solution)/shard_map/psum | solution.py:34
  375.1 0.0 copy-done.2
  375.1 0.0 copy-start
  375.1 9.4 %multiply_reduce_fusion = f32[]{:T(128)} fusion(f32[1024,3584]{0,1:T(8,128)} %convert_reduce_fusion, f32[]{:T(128)} %div.42, f32[3584]{0:T(1024)S(1)} %multiply_add_fusion.1, f32[1024]{0:T(1024)S(1)} %get-tuple-element.13), kind=kLoop, calls=%fused_computation.3 | loop fusion | flops 18350080 | bytes 14698504 | tf_op jit(solution)/shard_map/reduce_sum | solution.py:39
  384.5 46.3 %psum.31 = f32[]{:T(128)} all-reduce(f32[]{:T(128)} %multiply_reduce_fusion), channel_id=1, replica_groups=mesh['dp'=8,'tensor'=4] {'dp','tensor'}, use_global_device_ids=true, to_apply=%region_8.9 | all-reduce | flops 1 | bytes 8 | tf_op jit(solution)/shard_map/psum | solution.py:39
  431.6 11.3 %broadcast_divide_fusion = f32[1024,3584]{0,1:T(8,128)} fusion(f32[]{:T(128)S(6)} %max_shard_map.3, f32[1024,3584]{0,1:T(8,128)} %convert_reduce_fusion, f32[]{:T(128)} %div.42, f32[3584]{0:T(1024)S(1)} %multiply_add_fusion.1, f32[1024]{0:T(1024)S(1)} %get-tuple-element.13), kind=kLoop, calls=%fused_computation.8 | loop fusion | flops 14680064 | bytes 29378568 | tf_op jit(solution)/shard_map/div | solution.py:41
  442.9 0.0 copy-done.1
  442.9 0.0 copy-done
  442.9 14.3 %copy.14 = f32[1024,3584]{1,0:T(8,128)} copy(f32[1024,3584]{0,1:T(8,128)} %broadcast_divide_fusion) | data formatting | bytes 29360128
  (4 shorter events, 0.0 us)
Async XLA Ops:
  7.2 66.4 %all-gather.5.cloned.1.call-start = ((), (), s32[]{:S(2)}) async-start(), calls=%async_computation.2 | async-start | bytes 5242880 | tf_op jit(solution)/shard_map/all_gather | solution.py:19
  38.2 237.0 %all-gather.3.cloned.1.call-start = ((), (), s32[]{:S(2)}) async-start(), calls=%async_computation.1 | async-start | bytes 16515072 | tf_op jit(solution)/shard_map/all_gather | solution.py:23
  328.0 13.5 %copy-start.3 = (f32[1024]{0:T(1024)S(1)}, f32[1024]{0:T(1024)}, u32[]{:S(2)}) copy-start(f32[1024]{0:T(1024)} %param.8) | copy-start | bytes 12292
  328.0 47.1 %copy-start.2 = (f32[3584]{0:T(1024)S(1)}, f32[3584]{0:T(1024)}, u32[]{:S(2)}) copy-start(f32[3584]{0:T(1024)} %param.9) | copy-start | bytes 43012
  342.1 100.7 %copy-start.1 = (f32[1024]{0:T(1024)}, f32[1024]{0:T(1024)S(1)}, u32[]{:S(2)}) copy-start(f32[1024]{0:T(1024)S(1)} %get-tuple-element.13) | copy-start | bytes 12292
  375.1 67.8 %copy-start = (f32[3584]{0:T(1024)}, f32[3584]{0:T(1024)S(1)}, u32[]{:S(2)}) copy-start(f32[3584]{0:T(1024)S(1)} %multiply_add_fusion.1) | copy-start | bytes 43012
Sparse Core Ops, SparseCore 0:
  38.4 35.1 all-gather.4
  76.3 198.8 all-gather.2
where the time goes:
time: 466 us; the launch traced here: 465 us
  waiting for transfers between devices  233 us (50%)
  blocking collectives  114 us (24%)
  other arithmetic  58.1 us (12%)
  matrix products  28 us (6%)
  between operations  16.6 us (4%)
  local copies, waits for them, and re-layouts  15.6 us (3%)
    all_gather x1, waiting for transfers between devices, shards(): incoming = lax.all_gather(hidden, 'dp', axis=0, tiled=True)  202 us
    psum x1, blocking collectives, shards(): square_total = lax.psum(jnp.sum(raw_update * raw_update), ('dp', 'tensor'))  46.3 us
    psum x1, blocking collectives, shards(): row_sum_all = lax.psum(jnp.sum(row_next), 'dp')  32.3 us
    all_gather x1, waiting for transfers between devices, shards(): tokens_all = lax.all_gather(spread, 'tensor', axis=0, tiled=True)  30.8 us
    all_to_all x1, blocking collectives, shards(): lax.all_to_all(cotangent, 'dp', split_axis=1, concat_axis=0, tiled=True)  29.7 us
    dot_general x1, matrix products, shards(): jnp.einsum('jntd,njtf->ndf', blocks, shaped, preferred_element_type=jnp.f...  28 us
    reduce_sum x1, other arithmetic, shards(): gradient = jnp.sum(rounded.astype(jnp.float32), axis=0)  24.8 us
    unnamed x9, local copies, waits for them, and re-layouts  14.3 us
  transfers between devices with their start and end apart: 2, of which 2 were waited for; matrix products, arithmetic and copies ran while one was open for 1% of the time, Pallas kernels for 0%

commit v1 on v0

--- a/solution.py
+++ b/solution.py
@@ -16,7 +16,14 @@
     data_count = lax.axis_size("dp")
     tensor_count = lax.axis_size("tensor")
     spread = lax.all_to_all(cotangent, "dp", split_axis=1, concat_axis=0, tiled=True)
-    tokens_all = lax.all_gather(spread, "tensor", axis=0, tiled=True)
+    ring = [spread]
+    for hop in range(3):
+        ring.append(lax.ppermute(ring[-1], "tensor", [(dev, (dev + 1) % 4) for dev in range(4)]))
+    tokens_all = jnp.roll(
+        jnp.concatenate(ring[::-1], axis=0),
+        (lax.axis_index("tensor") + 1) * ring[0].shape[0],
+        axis=0,
+    )
     rows_each = cotangent.shape[0]
     block_rows = hidden.shape[0]
     blocks = tokens_all.reshape(tensor_count, data_count, rows_each, tokens_all.shape[1])

time: 466 us -> 407 us (0.87)
  waiting for transfers between devices: 233 us -> 155 us
  blocking collectives: 114 us -> 140 us
  local copies, waits for them, and re-layouts: 15.6 us -> 6.91 us
    all_gather x1, waiting for transfers between devices: 202 us -> 112 us  [shards(): incoming = lax.all_gather(hidden, 'dp', axis=0, tiled=True)]
    ppermute x0 -> x3, waiting for transfers between devices: none -> 42.8 us  [shards(): lax.ppermute(ring[-1], 'tensor', [(dev, (dev + 1) % 4) for dev in range(4)])]
    all_gather x1 -> x0, waiting for transfers between devices: 30.8 us -> none  [shards(): tokens_all = lax.all_gather(spread, 'tensor', axis=0, tiled=True)]
    all_to_all x1, blocking collectives: 29.7 us -> 55.4 us  [shards(): lax.all_to_all(cotangent, 'dp', split_axis=1, concat_axis=0, tiled=True)]
    unnamed x9 -> x15, local copies, waits for them, and re-layouts: 14.3 us -> 3.06 us
  transfers between devices with their start and end apart: 2 -> 4, of which waited for: 2 -> 4; matrix products, arithmetic and copies ran while one was open for 1% -> 2% of each run, Pallas kernels for 0% -> 0%
where the time goes in v1:
time: 407 us
  waiting for transfers between devices  155 us (38%)
  blocking collectives  140 us (34%)
  other arithmetic  60.3 us (15%)
  matrix products  27.8 us (7%)
  between operations  16.6 us (4%)
  local copies, waits for them, and re-layouts  6.91 us (2%)
    all_gather x1, waiting for transfers between devices, shards(): incoming = lax.all_gather(hidden, 'dp', axis=0, tiled=True)  112 us
    all_to_all x1, blocking collectives, shards(): lax.all_to_all(cotangent, 'dp', split_axis=1, concat_axis=0, tiled=True)  55.4 us
    psum x1, blocking collectives, shards(): square_total = lax.psum(jnp.sum(raw_update * raw_update), ('dp', 'tensor'))  46.3 us
    ppermute x3, waiting for transfers between devices, shards(): lax.ppermute(ring[-1], 'tensor', [(dev, (dev + 1) % 4) for dev in range(4)])  42.8 us
    psum x1, blocking collectives, shards(): row_sum_all = lax.psum(jnp.sum(row_next), 'dp')  32.3 us
    dot_general x1, matrix products, shards(): jnp.einsum('jntd,njtf->ndf', blocks, shaped, preferred_element_type=jnp.f...  27.8 us
    reduce_sum x1, other arithmetic, shards(): gradient = jnp.sum(rounded.astype(jnp.float32), axis=0)  25.2 us
    div x1, other arithmetic, shards(): update = raw_update / jnp.maximum(1.0, norm_value)  11.2 us
  transfers between devices with their start and end apart: 4, of which 4 were waited for; matrix products, arithmetic and copies ran while one was open for 2% of the time, Pallas kernels for 0%

profile of v1, /device:TPU:12, one launch (start us, length us, event | category | flops | bytes accessed | tf_op | source)
XLA Modules:
  0.0 406.8 jit_solution(7014774828081869802)
XLA Ops:
  7.2 4.4 %fusion.7 = bf16[256,3584]{1,0:T(8,128)(2,1)} fusion(bf16[256,3584]{1,0:T(8,128)(2,1)} %param.7, bf16[256,3584]{1,0:T(8,128)(2,1)} %param.6), kind=kLoop, calls=%fused_computation.15 | loop fusion | flops 7340032 | bytes 5505024 | tf_op jit(solution)/shard_map/convert_element_type | solution.py:13
  11.6 1.3 copy.19
  13.0 55.4 %all_to_all.19 = bf16[64,8,1024]{2,0,1:T(8,128)(2,1)S(1)} all-to-all(bf16[64,8,1024]{2,0,1:T(8,128)(2,1)S(1)} %bitcast.17), channel_id=1, replica_groups=mesh['dp'=8,'tensor'=4] {'dp'}, dimensions={1} | all-to-all | bytes 2097152 | tf_op jit(solution)/shard_map/all_to_all | solution.py:18
  68.4 14.2 %collective-permute-done = bf16[512,1024]{1,0:T(8,128)(2,1)S(1)} collective-permute-done((bf16[512,1024]{1,0:T(8,128)(2,1)S(1)}, bf16[512,1024]{1,0:T(8,128)(2,1)S(1)}, u32[]{:S(2)}, u32[]{:S(2)}) %collective-permute-start) | collective-permute-done | bytes 1048608 | tf_op jit(solution)/shard_map/ppermute | solution.py:21
  82.6 14.2 %collective-permute-done.1 = bf16[512,1024]{1,0:T(8,128)(2,1)S(1)} collective-permute-done((bf16[512,1024]{1,0:T(8,128)(2,1)S(1)}, bf16[512,1024]{1,0:T(8,128)(2,1)S(1)}, u32[]{:S(2)}, u32[]{:S(2)}) %collective-permute-start.1) | collective-permute-done | bytes 1048608 | tf_op jit(solution)/shard_map/ppermute | solution.py:21
  96.8 14.3 %collective-permute-done.2 = bf16[512,1024]{1,0:T(8,128)(2,1)} collective-permute-done((bf16[512,1024]{1,0:T(8,128)(2,1)S(1)}, bf16[512,1024]{1,0:T(8,128)(2,1)}, u32[]{:S(2)}, u32[]{:S(2)}) %collective-permute-start.2) | collective-permute-done | bytes 1048608 | tf_op jit(solution)/shard_map/ppermute | solution.py:21
  111.2 1.4 constant_dynamic-update-slice_fusion.7
  112.6 0.1 constant_dynamic-update-slice_fusion.6
  112.6 0.1 constant_dynamic-update-slice_fusion.5
  112.7 0.1 constant_dynamic-update-slice_fusion.4
  112.8 1.3 constant_dynamic-update-slice_fusion.3
  114.1 0.1 constant_dynamic-update-slice_fusion.2
  114.2 0.1 constant_dynamic-update-slice_fusion.1
  114.3 2.5 constant_dynamic-slice_fusion
  116.8 112.4 %all-gather.2.cloned.1.call-done = bf16[2048,3584]{1,0:T(8,128)(2,1)} async-done(((bf16[256,3584]{1,0:T(8,128)(2,1)}), bf16[2048,3584]{1,0:T(8,128)(2,1)}) %all-gather.2.cloned.1.call-update) | async-done | bytes 14680080 | tf_op jit(solution)/shard_map/all_gather | solution.py:30
  229.2 27.8 %bitcast_convert_fusion = bf16[8,1024,3584]{2,1,0:T(8,128)(2,1)} fusion(bf16[4,8,64,1024]{3,2,1,0:T(8,128)(2,1)} %bitcast.16, bf16[8,4,64,3584]{3,2,1,0:T(8,128)(2,1)} %bitcast.19), kind=kOutput, calls=%fused_computation | convolution fusion | flops 15061745664 | bytes 77594624 | tf_op jit(solution)/shard_map/jntd,njtf->ndf/dot_general | solution.py:33
  257.0 25.2 %convert_reduce_fusion = f32[1024,3584]{1,0:T(8,128)} fusion(bf16[8,1024,3584]{2,1,0:T(8,128)(2,1)} %bitcast_convert_fusion), kind=kLoop, calls=%fused_computation.1 | loop fusion | flops 55050240 | bytes 73400320 | tf_op jit(solution)/shard_map/reduce_sum | solution.py:35
  282.2 10.6 %fusion.1 = (f32[3584]{0:T(1024)S(1)}, f32[1024]{0:T(1024)S(1)}) fusion(f32[1024,3584]{1,0:T(8,128)} %convert_reduce_fusion), kind=kLoop, calls=%fused_computation.6 | loop fusion | flops 14675456 | bytes 14698496 | tf_op jit(solution)/shard_map/reduce_sum | solution.py:37
  292.9 5.9 %psum.28 = f32[1024]{0:T(1024)S(1)} all-reduce(f32[1024]{0:T(1024)S(1)} %get-tuple-element.5), channel_id=1, replica_groups=mesh['dp'=8,'tensor'=4] {'tensor'}, use_global_device_ids=true, to_apply=%region_2.3 | all-reduce | flops 1024 | bytes 8192 | tf_op jit(solution)/shard_map/psum | solution.py:38
  298.7 0.6 fusion.8
  299.3 32.3 %all-reduce = (f32[]{:T(128)}, f32[3584]{0:T(1024)S(1)}) all-reduce(f32[]{:T(128)} %get-tuple-element.8, f32[3584]{0:T(1024)S(1)} %get-tuple-element.4), channel_id=1, replica_groups=mesh['dp'=8,'tensor'=4] {'dp'}, use_global_device_ids=true, to_apply=%region_6.7 | all-reduce | flops 3585 | bytes 28680 | tf_op jit(solution)/shard_map/psum | solution.py:41
  332.3 8.3 %multiply_reduce_fusion = f32[]{:T(128)} fusion(f32[1024,3584]{1,0:T(8,128)} %convert_reduce_fusion, f32[]{:T(128)} %div.42, f32[3584]{0:T(1024)S(1)} %multiply_add_fusion.1, f32[1024]{0:T(1024)S(1)} %get-tuple-element.9), kind=kLoop, calls=%fused_computation.3 | loop fusion | flops 18350080 | bytes 14698504 | tf_op jit(solution)/shard_map/reduce_sum | solution.py:46
  340.6 46.3 %psum.31 = f32[]{:T(128)} all-reduce(f32[]{:T(128)} %multiply_reduce_fusion), channel_id=1, replica_groups=mesh['dp'=8,'tensor'=4] {'dp','tensor'}, use_global_device_ids=true, to_apply=%region_8.9 | all-reduce | flops 1 | bytes 8 | tf_op jit(solution)/shard_map/psum | solution.py:46
  387.7 11.2 %broadcast_divide_fusion = f32[1024,3584]{1,0:T(8,128)} fusion(f32[]{:T(128)S(6)} %max_shard_map.3, f32[1024,3584]{1,0:T(8,128)} %convert_reduce_fusion, f32[]{:T(128)} %div.42, f32[3584]{0:T(1024)S(1)} %multiply_add_fusion.1, f32[1024]{0:T(1024)S(1)} %get-tuple-element.9), kind=kLoop, calls=%fused_computation.8 | loop fusion | flops 14680064 | bytes 29378568 | tf_op jit(solution)/shard_map/div | solution.py:48
  (15 shorter events, 0.2 us)
Async XLA Ops:
  7.2 222.1 %all-gather.2.cloned.1.call-start = ((), (), s32[]{:S(2)}) async-start(), calls=%async_computation.1 | async-start | bytes 16515072 | tf_op jit(solution)/shard_map/all_gather | solution.py:30
  68.4 14.2 %collective-permute-start = (bf16[512,1024]{1,0:T(8,128)(2,1)S(1)}, bf16[512,1024]{1,0:T(8,128)(2,1)S(1)}, u32[]{:S(2)}, u32[]{:S(2)}) collective-permute-start(bf16[512,1024]{1,0:T(8,128)(2,1)S(1)} %bitcast.13), channel_id=1, source_target_pairs={{0,1},{1,2},{2,3},{3,0},{4,5},{5,6},{6,7},{7,4},{8,9},{9,10},{10,1... | collective-permute-start | bytes 3145736 | tf_op jit(solution)/shard_map/ppermute | solution.py:21
  82.6 14.2 %collective-permute-start.1 = (bf16[512,1024]{1,0:T(8,128)(2,1)S(1)}, bf16[512,1024]{1,0:T(8,128)(2,1)S(1)}, u32[]{:S(2)}, u32[]{:S(2)}) collective-permute-start(bf16[512,1024]{1,0:T(8,128)(2,1)S(1)} %collective-permute-done), channel_id=1, source_target_pairs={{0,1},{1,2},{2,3},{3,0},{4,5},{5,6},{6,7},{7,4},{8,9},{9,10},{10,1... | collective-permute-start | bytes 3145736 | tf_op jit(solution)/shard_map/ppermute | solution.py:21
  96.8 14.3 %collective-permute-start.2 = (bf16[512,1024]{1,0:T(8,128)(2,1)S(1)}, bf16[512,1024]{1,0:T(8,128)(2,1)}, u32[]{:S(2)}, u32[]{:S(2)}) collective-permute-start(bf16[512,1024]{1,0:T(8,128)(2,1)S(1)} %collective-permute-done.1), channel_id=1, source_target_pairs={{0,1},{1,2},{2,3},{3,0},{4,5},{5,6},{6,7},{7,4},{8,9},{9,10},{10,1... | collective-permute-start | bytes 3145736 | tf_op jit(solution)/shard_map/ppermute | solution.py:21
  282.2 16.5 %copy-start.3 = (f32[1024]{0:T(1024)S(1)}, f32[1024]{0:T(1024)}, u32[]{:S(2)}) copy-start(f32[1024]{0:T(1024)} %param.8) | copy-start | bytes 12292
  282.2 50.0 %copy-start.2 = (f32[3584]{0:T(1024)S(1)}, f32[3584]{0:T(1024)}, u32[]{:S(2)}) copy-start(f32[3584]{0:T(1024)} %param.9) | copy-start | bytes 43012
  299.3 99.5 %copy-start.1 = (f32[1024]{0:T(1024)}, f32[1024]{0:T(1024)S(1)}, u32[]{:S(2)}) copy-start(f32[1024]{0:T(1024)S(1)} %get-tuple-element.9) | copy-start | bytes 12292
  332.3 66.6 %copy-start = (f32[3584]{0:T(1024)}, f32[3584]{0:T(1024)S(1)}, u32[]{:S(2)}) copy-start(f32[3584]{0:T(1024)S(1)} %multiply_add_fusion.1) | copy-start | bytes 43012
Sparse Core Ops, SparseCore 0:
  11.8 217.4 all-gather.1
